TPU v7x, 256 devices: a whole 4x4x8 slice. The times are simulated.
256 devices in a mesh: dp: 32 (over z, y_hi, core), mp: 8 (over x, y_lo).
Axes of the slice: x: 4, y: 4 (y_hi: 2, y_lo: 2; y = y_hi * 2 + y_lo), z: 8, core: 2. Of those that a mesh axis runs over, the one named last changes fastest.
Arguments:
- activations: bfloat16 [16384, 28672], P('dp', 'mp'), may hold values from -200 to 200
- weight: bfloat16 [8192, 28672], P(None, ('mp', 'dp')), may hold values from -25 to 25
- thresholds: float32 [8192], P('dp'), may hold values from 0.5 to 1.5
Outputs:
- pruned: bfloat16 [8192, 28672], P('dp', 'mp')
All inputs are finite; a program needn't handle non-finite values.
Results may differ from a plain program's by a relative error of at most 0.0004.
Values may be sent and summed in bfloat16 or wider, within the bound.
A program may use at most 64 MiB of HBM per device.

v0:
```python
import jax
import jax.numpy as jnp
from jax import lax
from jax.sharding import PartitionSpec as P

IN = 28672
gate_slope = 2.0
small_eps = 1e-06


def sent_to_all(shard, axis):
    copies = jnp.broadcast_to(shard, (lax.axis_size(axis), *shard.shape))
    return lax.all_to_all(copies, axis, split_axis=0, concat_axis=0, tiled=True)


def over_copies(shard, axis):
    return sent_to_all(shard, axis).sum(axis=0)


def soft_prune(block, col_norm, row_total, limit):
    wide = block.astype(jnp.float32)
    scores = jnp.abs(wide) * col_norm[None, :]
    row_mean = row_total[:, None] / IN + small_eps
    kept_share = jnp.clip((scores / row_mean - limit[:, None]) * gate_slope + 0.5, 0.0, 1.0)
    return (wide * kept_share).astype(jnp.bfloat16)


def per_device(activations, weight, thresholds):
    partial_value = jnp.sum(jnp.square(activations.astype(jnp.float32)), axis=0)
    relaid = lax.all_to_all(weight, "dp", split_axis=0, concat_axis=1, tiled=True)
    squares = over_copies(partial_value, "dp")
    col_norm = jnp.sqrt(squares)
    row_part = jnp.sum(jnp.abs(relaid.astype(jnp.float32)) * col_norm[None, :], axis=1)
    row_total = over_copies(row_part, "mp")
    return soft_prune(relaid, col_norm, row_total, thresholds)


def solution(mesh):
    placed = (P("dp", "mp"), P(None, ("mp", "dp")), P("dp"))
    return jax.shard_map(
        per_device, mesh=mesh, in_specs=placed, out_specs=P("dp", "mp"), check_vma=False
    )
```

profile of v0, /device:TPU:16, one launch (start us, length us, event | category | flops | bytes accessed | tf_op | source)
XLA Modules:
  0.0 99.5 jit_solution(1914880998920261515)
XLA Ops:
  0.0 0.0 copy-start
  0.0 2.9 %multiply_reduce_fusion = f32[3584]{0:T(1024)S(1)} fusion(bf16[512,3584]{1,0:T(8,128)(2,1)} %param.3), kind=kLoop, calls=%fused_computation | loop fusion | flops 5501440 | bytes 3684352 | tf_op jit(solution)/shard_map/reduce_sum | solution.py:29
  2.9 1.0 %broadcast_in_dim.4 = f32[32,1,3584]{2,1,0:T(1,128)} broadcast(f32[3584]{0:T(1024)S(1)} %multiply_reduce_fusion), dimensions={2} | broadcast | bytes 473088 | tf_op jit(solution)/shard_map/broadcast_in_dim | solution.py:12
  3.9 11.6 %all-to-all-start.1 = ((f32[32,1,3584]{2,1,0:T(1,128)}), f32[32,1,3584]{2,1,0:T(1,128)S(1)}, u32[]{:S(2)}, u32[]{:S(2)}) async-start(f32[32,1,3584]{2,1,0:T(1,128)} %broadcast_in_dim.4), calls=%async_computation.1 | async-start | bytes 917504 | tf_op jit(solution)/shard_map/all_to_all | solution.py:13
  15.5 0.0 copy-done
  15.5 1.4 %copy.23 = bf16[14,32,8,256]{3,2,0,1:T(8,128)(2,1)} copy(bf16[14,32,8,256]{3,2,1,0:T(8,128)(2,1)S(1)} %bitcast.26) | data formatting | bytes 3670016 | tf_op jit(solution)/shard_map/all_to_all | solution.py:30
  16.9 0.0 copy-start.1
  16.9 14.9 %all-to-all-done.1 = f32[32,1,3584]{2,1,0:T(1,128)S(1)} async-done(((f32[32,1,3584]{2,1,0:T(1,128)}), f32[32,1,3584]{2,1,0:T(1,128)S(1)}, u32[]{:S(2)}, u32[]{:S(2)}) %all-to-all-start.1) | async-done | bytes 458784 | tf_op jit(solution)/shard_map/all_to_all | solution.py:13
  31.8 5.0 %all-to-all-start = ((bf16[32,256,112]{1,2,0:T(8,128)(2,1)}), bf16[32,256,112]{1,2,0:T(8,128)(2,1)S(1)}, u32[]{:S(2)}, u32[]{:S(2)}) async-start(bf16[32,256,112]{1,2,0:T(8,128)(2,1)} %bitcast.25), calls=%async_computation | async-start | bytes 3670016 | tf_op jit(solution)/shard_map/all_to_all | solution.py:30
  36.8 0.3 reduce_sum.37
  37.1 0.1 sqrt.12
  37.2 44.3 %all-to-all-done = bf16[32,256,112]{1,2,0:T(8,128)(2,1)S(1)} async-done(((bf16[32,256,112]{1,2,0:T(8,128)(2,1)}), bf16[32,256,112]{1,2,0:T(8,128)(2,1)S(1)}, u32[]{:S(2)}, u32[]{:S(2)}) %all-to-all-start) | async-done | bytes 1835040 | tf_op jit(solution)/shard_map/all_to_all | solution.py:30
  81.5 0.6 fusion.1
  82.0 11.0 %all_to_all.25 = f32[8,1,256]{2,1,0:T(1,128)S(1)} all-to-all(f32[8,1,256]{2,1,0:T(1,128)S(1)} %broadcast_in_dim.5), channel_id=1, replica_groups=mesh['dp'=32,'mp'=8] {'mp'}, dimensions={0} | all-to-all | bytes 16384 | tf_op jit(solution)/shard_map/all_to_all | solution.py:13
  93.1 0.0 copy-done.1
  93.1 2.6 %fusion.8 = bf16[256,3584]{0,1:T(8,128)(2,1)} fusion(bf16[32,256,112]{1,2,0:T(8,128)(2,1)S(1)} %all-to-all-done, f32[256]{0:T(256)S(1)} %copy-done.1, f32[256]{0:T(256)S(1)} %multiply_add_fusion, f32[3584]{0:T(1024)S(1)} %sqrt.11), kind=kLoop, calls=%fused_computation.12 | loop fusion | flops 9175040 | bytes 3686400 | tf_op jit(solution)/shard_map/convert_element_type | solution.py:25
  95.7 3.8 %copy.18 = bf16[256,3584]{1,0:T(8,128)(2,1)} copy(bf16[256,3584]{0,1:T(8,128)(2,1)} %fusion.8) | data formatting | bytes 3670016 | tf_op jit(solution)/shard_map/convert_element_type | solution.py:25
  (4 shorter events, 0.1 us)
Async XLA Ops:
  0.0 15.5 %copy-start = (bf16[8192,112]{0,1:T(8,128)(2,1)S(1)}, bf16[8192,112]{0,1:T(8,128)(2,1)}, u32[]{:S(2)}) copy-start(bf16[8192,112]{0,1:T(8,128)(2,1)} %param.4) | copy-start | bytes 5505028
  3.9 27.9 %all-to-all-start.1 = ((f32[32,1,3584]{2,1,0:T(1,128)}), f32[32,1,3584]{2,1,0:T(1,128)S(1)}, u32[]{:S(2)}, u32[]{:S(2)}) async-start(f32[32,1,3584]{2,1,0:T(1,128)} %broadcast_in_dim.4), calls=%async_computation.1 | async-start | bytes 917504 | tf_op jit(solution)/shard_map/all_to_all | solution.py:13
  16.9 76.2 %copy-start.1 = (f32[256]{0:T(256)S(1)}, f32[256]{0:T(256)}, u32[]{:S(2)}) copy-start(f32[256]{0:T(256)} %param.5) | copy-start | bytes 3076
  31.8 49.7 %all-to-all-start = ((bf16[32,256,112]{1,2,0:T(8,128)(2,1)}), bf16[32,256,112]{1,2,0:T(8,128)(2,1)S(1)}, u32[]{:S(2)}, u32[]{:S(2)}) async-start(bf16[32,256,112]{1,2,0:T(8,128)(2,1)} %bitcast.25), calls=%async_computation | async-start | bytes 3670016 | tf_op jit(solution)/shard_map/all_to_all | solution.py:30
where the time goes:
time: 99.9 us; the launch traced here: 99.5 us
  waiting for transfers between devices  59.2 us (59%)
  starting transfers between devices  16.6 us (17%)
  blocking collectives  11 us (11%)
  other arithmetic  6.43 us (6%)
  local copies, waits for them, and re-layouts  6.26 us (6%)
    all_to_all x1, waiting for transfers between devices, per_device(): lax.all_to_all(weight, 'dp', split_axis=0, concat_axis=1, tiled=True)  44.3 us
    all_to_all x1, waiting for transfers between devices, sent_to_all(): return lax.all_to_all(copies, axis, split_axis=0, concat_axis=0, tiled=True)  14.9 us
    all_to_all x1, starting transfers between devices, sent_to_all(): return lax.all_to_all(copies, axis, split_axis=0, concat_axis=0, tiled=True)  11.6 us
    all_to_all x1, blocking collectives, sent_to_all(): return lax.all_to_all(copies, axis, split_axis=0, concat_axis=0, tiled=True)  11 us
    all_to_all x1, starting transfers between devices, per_device(): lax.all_to_all(weight, 'dp', split_axis=0, concat_axis=1, tiled=True)  4.99 us
    convert_element_type x1, local copies, waits for them, and re-layouts, soft_prune(): return (wide * kept_share).astype(jnp.bfloat16)  3.8 us
    reduce_sum x1, other arithmetic, per_device(): partial_value = jnp.sum(jnp.square(activations.astype(jnp.float32)), axis=0)  2.92 us
    convert_element_type x1, other arithmetic, soft_prune(): return (wide * kept_share).astype(jnp.bfloat16)  2.65 us
  transfers between devices with their start and end apart: 2, of which 2 were waited for; matrix products, arithmetic and copies ran while one was open for 2% of the time, Pallas kernels for 0%

commit v1 on v0

--- a/solution.py
+++ b/solution.py
@@ -27,7 +27,9 @@
 
 def per_device(activations, weight, thresholds):
     partial_value = jnp.sum(jnp.square(activations.astype(jnp.float32)), axis=0)
-    relaid = lax.all_to_all(weight, "dp", split_axis=0, concat_axis=1, tiled=True)
+    pieces = jnp.split(weight, lax.axis_size("dp"), axis=0)
+    received = lax.all_to_all(jnp.stack(pieces), "dp", 0, 0)
+    relaid = jnp.concatenate(received, axis=1)
     squares = over_copies(partial_value, "dp")
     col_norm = jnp.sqrt(squares)
     row_part = jnp.sum(jnp.abs(relaid.astype(jnp.float32)) * col_norm[None, :], axis=1)

time: 99.9 us -> 117 us (1.17)
  local copies, waits for them, and re-layouts: 6.26 us -> 32.5 us
  waiting for transfers between devices: 59.2 us -> 44.3 us
  starting transfers between devices: 16.6 us -> 21.4 us
    unnamed x4 -> x35, local copies, waits for them, and re-layouts: 0.01 us -> 26.7 us
    all_to_all x1, waiting for transfers between devices: 14.9 us -> 0.01 us  [sent_to_all(): return lax.all_to_all(copies, axis, split_axis=0, concat_axis=0, tiled=True)]
    all_to_all x1, starting transfers between devices: 4.99 us -> 9.78 us  [per_device(): received = lax.all_to_all(jnp.stack(pieces), 'dp', 0, 0)]
    all_to_all x1 -> x0, local copies, waits for them, and re-layouts: 1.35 us -> none  [per_device(): lax.all_to_all(weight, 'dp', split_axis=0, concat_axis=1, tiled=True)]
  transfers between devices with their start and end apart: 2 -> 2, of which waited for: 2 -> 1; matrix products, arithmetic and copies ran while one was open for 2% -> 23% of each run, Pallas kernels for 0% -> 0%
where the time goes in v1:
time: 117 us; the launch traced here: 115 us
  waiting for transfers between devices  44.3 us (38%)
  local copies, waits for them, and re-layouts  32.5 us (28%)
  starting transfers between devices  21.4 us (18%)
  blocking collectives  11 us (9%)
  other arithmetic  6.29 us (5%)
    all_to_all x1, waiting for transfers between devices, per_device(): received = lax.all_to_all(jnp.stack(pieces), 'dp', 0, 0)  44.3 us
    unnamed x35, local copies, waits for them, and re-layouts  26.7 us
    all_to_all x1, starting transfers between devices, sent_to_all(): return lax.all_to_all(copies, axis, split_axis=0, concat_axis=0, tiled=True)  11.6 us
    all_to_all x1, blocking collectives, sent_to_all(): return lax.all_to_all(copies, axis, split_axis=0, concat_axis=0, tiled=True)  11 us
    all_to_all x1, starting transfers between devices, per_device(): received = lax.all_to_all(jnp.stack(pieces), 'dp', 0, 0)  9.78 us
    convert_element_type x1, local copies, waits for them, and re-layouts, soft_prune(): return (wide * kept_share).astype(jnp.bfloat16)  3.8 us
    reduce_sum x1, other arithmetic, per_device(): partial_value = jnp.sum(jnp.square(activations.astype(jnp.float32)), axis=0)  2.79 us
    convert_element_type x1, other arithmetic, soft_prune(): return (wide * kept_share).astype(jnp.bfloat16)  2.65 us
  transfers between devices with their start and end apart: 2, of which 1 were waited for; matrix products, arithmetic and copies ran while one was open for 23% of the time, Pallas kernels for 0%

profile of v1, /device:TPU:16, one launch (start us, length us, event | category | flops | bytes accessed | tf_op | source)
XLA Modules:
  0.0 115.5 jit_solution(5318130908527269115)
XLA Ops:
  0.0 2.8 %multiply_reduce_fusion = f32[3584]{0:T(1024)S(1)} fusion(bf16[512,3584]{1,0:T(8,128)(2,1)} %param.3), kind=kLoop, calls=%fused_computation | loop fusion | flops 5501440 | bytes 3684352 | tf_op jit(solution)/shard_map/reduce_sum | solution.py:29
  2.8 1.0 broadcast_in_dim.4
  3.8 11.6 %all-to-all-start.1 = ((f32[32,1,3584]{2,1,0:T(1,128)}), f32[32,1,3584]{2,1,0:T(1,128)S(1)}, u32[]{:S(2)}, u32[]{:S(2)}) async-start(f32[32,1,3584]{2,1,0:T(1,128)} %broadcast_in_dim.4), calls=%async_computation.1 | async-start | bytes 917504 | tf_op jit(solution)/shard_map/all_to_all | solution.py:13
  15.4 0.8 constant_dynamic-update-slice_fusion.31
  16.2 0.8 constant_dynamic-update-slice_fusion.30
  17.0 0.8 constant_dynamic-update-slice_fusion.29
  17.9 0.8 constant_dynamic-update-slice_fusion.28
  18.7 0.8 constant_dynamic-update-slice_fusion.27
  19.5 0.8 constant_dynamic-update-slice_fusion.26
  20.3 0.8 constant_dynamic-update-slice_fusion.25
  21.2 0.8 constant_dynamic-update-slice_fusion.24
  22.0 0.8 constant_dynamic-update-slice_fusion.23
  22.8 0.8 constant_dynamic-update-slice_fusion.22
  23.6 0.8 constant_dynamic-update-slice_fusion.21
  24.4 0.8 constant_dynamic-update-slice_fusion.20
  25.3 0.8 constant_dynamic-update-slice_fusion.19
  26.1 0.8 constant_dynamic-update-slice_fusion.18
  26.9 0.8 constant_dynamic-update-slice_fusion.17
  27.7 0.8 constant_dynamic-update-slice_fusion.16
  28.6 0.8 constant_dynamic-update-slice_fusion.15
  29.4 0.8 constant_dynamic-update-slice_fusion.14
  30.2 0.8 constant_dynamic-update-slice_fusion.13
  31.0 0.8 constant_dynamic-update-slice_fusion.12
  31.9 0.8 constant_dynamic-update-slice_fusion.11
  32.7 0.8 constant_dynamic-update-slice_fusion.10
  33.5 0.8 constant_dynamic-update-slice_fusion.9
  34.3 0.8 constant_dynamic-update-slice_fusion.8
  35.1 0.8 constant_dynamic-update-slice_fusion.7
  36.0 0.8 constant_dynamic-update-slice_fusion.6
  36.8 0.8 constant_dynamic-update-slice_fusion.5
  37.6 0.8 constant_dynamic-update-slice_fusion.4
  38.4 0.8 constant_dynamic-update-slice_fusion.3
  39.3 0.8 constant_dynamic-update-slice_fusion.2
  40.1 0.8 constant_dynamic-update-slice_fusion.1
  40.9 0.8 constant_dynamic-update-slice_fusion
  41.7 0.0 copy-start
  41.7 1.2 %copy-done = bf16[32,256,112]{1,2,0:T(8,128)(2,1)} copy-done((bf16[32,256,112]{1,2,0:T(8,128)(2,1)}, bf16[32,256,112]{1,2,0:T(8,128)(2,1)S(1)}, u32[]{:S(2)}) %copy-start) | copy-done | bytes 1835032
  43.0 0.0 all-to-all-done.1
  43.0 9.8 %all-to-all-start = ((bf16[32,256,112]{1,2,0:T(8,128)(2,1)}), bf16[32,256,112]{1,2,0:T(8,128)(2,1)S(1)}, u32[]{:S(2)}, u32[]{:S(2)}) async-start(bf16[32,256,112]{1,2,0:T(8,128)(2,1)} %copy-done), calls=%async_computation | async-start | bytes 3670016 | tf_op jit(solution)/shard_map/all_to_all | solution.py:31
  52.7 0.0 copy-start.1
  52.8 0.3 reduce_sum.37
  53.1 0.1 sqrt.12
  53.1 44.3 %all-to-all-done = bf16[32,256,112]{1,2,0:T(8,128)(2,1)S(1)} async-done(((bf16[32,256,112]{1,2,0:T(8,128)(2,1)}), bf16[32,256,112]{1,2,0:T(8,128)(2,1)S(1)}, u32[]{:S(2)}, u32[]{:S(2)}) %all-to-all-start) | async-done | bytes 1835040 | tf_op jit(solution)/shard_map/all_to_all | solution.py:31
  97.4 0.6 fusion.1
  98.0 11.0 %all_to_all.17 = f32[8,1,256]{2,1,0:T(1,128)S(1)} all-to-all(f32[8,1,256]{2,1,0:T(1,128)S(1)} %broadcast_in_dim.5), channel_id=1, replica_groups=mesh['dp'=32,'mp'=8] {'mp'}, dimensions={0} | all-to-all | bytes 16384 | tf_op jit(solution)/shard_map/all_to_all | solution.py:13
  109.0 0.0 copy-done.1
  109.0 2.6 %fusion.8 = bf16[256,3584]{0,1:T(8,128)(2,1)} fusion(bf16[32,256,112]{1,2,0:T(8,128)(2,1)S(1)} %all-to-all-done, f32[256]{0:T(256)S(1)} %copy-done.1, f32[256]{0:T(256)S(1)} %multiply_add_fusion, f32[3584]{0:T(1024)S(1)} %sqrt.11), kind=kLoop, calls=%fused_computation.12 | loop fusion | flops 9175040 | bytes 3686400 | tf_op jit(solution)/shard_map/convert_element_type | solution.py:25
  111.7 3.8 %copy.9 = bf16[256,3584]{1,0:T(8,128)(2,1)} copy(bf16[256,3584]{0,1:T(8,128)(2,1)} %fusion.8) | data formatting | bytes 3670016 | tf_op jit(solution)/shard_map/convert_element_type | solution.py:25
  (4 shorter events, 0.1 us)
Async XLA Ops:
  3.8 39.2 %all-to-all-start.1 = ((f32[32,1,3584]{2,1,0:T(1,128)}), f32[32,1,3584]{2,1,0:T(1,128)S(1)}, u32[]{:S(2)}, u32[]{:S(2)}) async-start(f32[32,1,3584]{2,1,0:T(1,128)} %broadcast_in_dim.4), calls=%async_computation.1 | async-start | bytes 917504 | tf_op jit(solution)/shard_map/all_to_all | solution.py:13
  41.7 1.2 %copy-start = (bf16[32,256,112]{1,2,0:T(8,128)(2,1)}, bf16[32,256,112]{1,2,0:T(8,128)(2,1)S(1)}, u32[]{:S(2)}) copy-start(bf16[32,256,112]{1,2,0:T(8,128)(2,1)S(1)} %constant_dynamic-update-slice_fusion) | copy-start | bytes 5505028
  43.0 54.5 %all-to-all-start = ((bf16[32,256,112]{1,2,0:T(8,128)(2,1)}), bf16[32,256,112]{1,2,0:T(8,128)(2,1)S(1)}, u32[]{:S(2)}, u32[]{:S(2)}) async-start(bf16[32,256,112]{1,2,0:T(8,128)(2,1)} %copy-done), calls=%async_computation | async-start | bytes 3670016 | tf_op jit(solution)/shard_map/all_to_all | solution.py:31
  52.7 56.3 %copy-start.1 = (f32[256]{0:T(256)S(1)}, f32[256]{0:T(256)}, u32[]{:S(2)}) copy-start(f32[256]{0:T(256)} %param.5) | copy-start | bytes 3076
